TPU v7x, 32 devices: a 4x4x1 block of a 4x4x8 slice. The times are simulated.
32 devices in a mesh: dp: 1 (over z), tp: 32 (over y, x, core).
Axes of the slice: x: 4, y: 4, z: 1, core: 2. Of those that a mesh axis runs over, the one named last changes fastest.
The devices are a block of a 4x4x8 slice.
Arguments:
- hidden: bfloat16 [8192, 1024], P(('dp', 'tp'))
- norm_gain: float32 [1024], replicated
- w_query: bfloat16 [1024, 128, 128], P(None, 'tp')
- w_key: bfloat16 [1024, 128, 128], P(None, 'tp')
- w_value: bfloat16 [1024, 128, 128], P(None, 'tp')
Outputs:
- output 1: bfloat16 [8192, 128, 128], P('dp', 'tp')
- output 2: bfloat16 [8192, 128, 128], P('dp', 'tp')
- output 3: bfloat16 [8192, 128, 128], P('dp', 'tp')
All inputs are finite; a program needn't handle non-finite values.
Results may differ from a plain program's by a relative error of at most 0.001.
Values are sent between devices in bfloat16 or wider.
A program may use at most 768 MiB of HBM per device.

v0:
```python
import jax
import jax.numpy as jnp
from jax import lax
from jax.sharding import PartitionSpec as P


def solution(mesh):
    def local_step(hidden_blk, norm_gain, wq_local, wk_local, wv_local):
        hidden_f32 = hidden_blk.astype(jnp.float32)
        mean_sq = jnp.mean(hidden_f32 * hidden_f32, axis=-1, keepdims=True)
        normed = (hidden_f32 * lax.rsqrt(mean_sq + 1e-6) * norm_gain).astype(jnp.bfloat16)
        gathered = lax.all_gather(normed, "tp", axis=0, tiled=True)
        q_out = jnp.einsum("td,dhk->thk", gathered, wq_local, preferred_element_type=jnp.float32).astype(jnp.bfloat16)
        k_out = jnp.einsum("td,dhk->thk", gathered, wk_local, preferred_element_type=jnp.float32).astype(jnp.bfloat16)
        v_out = jnp.einsum("td,dhk->thk", gathered, wv_local, preferred_element_type=jnp.float32).astype(jnp.bfloat16)
        return q_out, k_out, v_out

    row_spec = P(("dp", "tp"), None)
    head_spec = P(None, "tp", None)
    out_spec = P("dp", "tp", None)
    return jax.shard_map(local_step, mesh=mesh, in_specs=(row_spec, P(None), head_spec, head_spec, head_spec), out_specs=(out_spec, out_spec, out_spec), check_vma=False)
```

profile of v0, /device:TPU:97, one launch (start us, length us, event | category | flops | bytes accessed | tf_op | source)
XLA Modules:
  0.0 246.6 jit_solution(3067634450414156510)
XLA Ops:
  7.2 0.0 copy-start
  7.2 0.1 all-gather.2.cloned.1.call-start
  7.3 1.3 fusion.15
  8.6 2.0 fusion.17
  10.6 0.1 all-gather.2.cloned.1.call-update
  10.7 0.0 copy-start.2
  10.7 71.7 %all-gather.2.cloned.1.call-done = bf16[8192,1024]{1,0:T(8,128)(2,1)} async-done(((bf16[256,1024]{1,0:T(8,128)(2,1)}), bf16[8192,1024]{1,0:T(8,128)(2,1)}) %all-gather.2.cloned.1.call-update) | async-done | bytes 16777232 | tf_op jit(solution)/shard_map/all_gather | solution.py:12
  82.3 0.0 copy-done
  82.3 12.5 %fusion.9 = bf16[8192,4,128]{2,0,1:T(8,128)(2,1)S(1)} fusion(bf16[8192,1024]{1,0:T(8,128)(2,1)} %all-gather.2.cloned.1.call-done, bf16[1024,4,128]{2,1,0:T(4,128)(2,1)S(1)} %copy-done), kind=kOutput, calls=%fused_computation.7 | convolution fusion | flops 8594128896 | bytes 26214400 | tf_op jit(solution)/shard_map/td,dhk->thk/dot_general | solution.py:14
  94.8 39.9 %copy.12 = bf16[8192,4,128]{2,1,0:T(4,128)(2,1)} copy(bf16[8192,4,128]{2,0,1:T(8,128)(2,1)S(1)} %fusion.9) | data formatting | bytes 16777216
  134.8 0.0 copy-done.2
  134.8 12.5 %fusion.6 = bf16[8192,4,128]{2,0,1:T(8,128)(2,1)S(1)} fusion(bf16[8192,1024]{1,0:T(8,128)(2,1)} %all-gather.2.cloned.1.call-done, bf16[1024,4,128]{2,1,0:T(4,128)(2,1)S(1)} %copy-done.2), kind=kOutput, calls=%fused_computation.6 | convolution fusion | flops 8594128896 | bytes 26214400 | tf_op jit(solution)/shard_map/td,dhk->thk/dot_general | solution.py:13
  147.3 0.0 copy-start.3
  147.3 39.9 %copy.11 = bf16[8192,4,128]{2,1,0:T(4,128)(2,1)} copy(bf16[8192,4,128]{2,0,1:T(8,128)(2,1)S(1)} %fusion.6) | data formatting | bytes 16777216
  187.2 0.0 copy-done.3
  187.2 0.0 copy-start.1
  187.2 12.6 %fusion.12 = bf16[8192,4,128]{2,0,1:T(8,128)(2,1)S(1)} fusion(bf16[8192,1024]{1,0:T(8,128)(2,1)} %all-gather.2.cloned.1.call-done, bf16[1024,4,128]{2,1,0:T(4,128)(2,1)S(1)} %copy-done.3), kind=kOutput, calls=%fused_computation.8 | convolution fusion | flops 8594128896 | bytes 26214400 | tf_op jit(solution)/shard_map/td,dhk->thk/dot_general | solution.py:15
  199.8 39.9 %copy.13 = bf16[8192,4,128]{2,1,0:T(4,128)(2,1)} copy(bf16[8192,4,128]{2,0,1:T(8,128)(2,1)S(1)} %fusion.12) | data formatting | bytes 16777216
  239.7 0.0 copy-done.1
  (1 shorter events, 0.0 us)
Async XLA Ops:
  7.2 75.2 %copy-start = (bf16[1024,4,128]{2,1,0:T(4,128)(2,1)S(1)}, bf16[1024,4,128]{2,1,0:T(4,128)(2,1)}, u32[]{:S(2)}) copy-start(bf16[1024,4,128]{2,1,0:T(4,128)(2,1)} %param.8) | copy-start | bytes 3145732
  7.2 75.1 %all-gather.2.cloned.1.call-start = ((), (), s32[]{:S(2)}) async-start(), calls=%async_computation | async-start | bytes 17301504 | tf_op jit(solution)/shard_map/all_gather | solution.py:12
  10.7 124.1 %copy-start.2 = (bf16[1024,4,128]{2,1,0:T(4,128)(2,1)S(1)}, bf16[1024,4,128]{2,1,0:T(4,128)(2,1)}, u32[]{:S(2)}) copy-start(bf16[1024,4,128]{2,1,0:T(4,128)(2,1)} %param.7) | copy-start | bytes 3145732
  147.3 39.9 %copy-start.3 = (bf16[1024,4,128]{2,1,0:T(4,128)(2,1)S(1)}, bf16[1024,4,128]{2,1,0:T(4,128)(2,1)}, u32[]{:S(2)}) copy-start(bf16[1024,4,128]{2,1,0:T(4,128)(2,1)} %param.9) | copy-start | bytes 3145732
  187.2 52.5 %copy-start.1 = (bf16[1024,4,128]{2,1,0:T(4,128)(2,1)S(1)}, bf16[1024,4,128]{2,1,0:T(4,128)(2,1)}, u32[]{:S(2)}) copy-start(bf16[1024,4,128]{2,1,0:T(4,128)(2,1)} %param.8) | copy-start | bytes 3145732
Sparse Core Ops, SparseCore 0:
  10.8 71.5 all-gather.1
where the time goes:
time: 247 us
  local copies, waits for them, and re-layouts  120 us (49%)
  waiting for transfers between devices  71.7 us (29%)
  matrix products  37.6 us (15%)
  between operations  14.1 us (6%)
  other arithmetic  3.34 us (1%)
    unnamed x11, local copies, waits for them, and re-layouts  120 us
    all_gather x1, waiting for transfers between devices, local_step(): gathered = lax.all_gather(normed, 'tp', axis=0, tiled=True)  71.7 us
    dot_general x1, matrix products, local_step(): jnp.einsum('td,dhk->thk', gathered, wv_local, preferred_element_type=jnp....  12.6 us
    dot_general x1, matrix products, local_step(): jnp.einsum('td,dhk->thk', gathered, wq_local, preferred_element_type=jnp....  12.5 us
    dot_general x1, matrix products, local_step(): jnp.einsum('td,dhk->thk', gathered, wk_local, preferred_element_type=jnp....  12.5 us
  transfers between devices with their start and end apart: 1, of which 1 were waited for; matrix products, arithmetic and copies ran while one was open for 0% of the time, Pallas kernels for 0%

commit v1 on v0

v1 whole, which is shorter than its diff:
```python
import functools
import math

import jax
import jax.numpy as jnp
from jax import lax
from jax.experimental import pallas as pl
from jax.experimental.pallas import tpu as pltpu
from jax.sharding import PartitionSpec as P

MESH = pl.DeviceIdType.MESH
CORES = 2
LANES = 128

ORDER = ((0, 0), (-1, 0), (1, 0), (0, -1), (0, 1), (2, 0), (-1, -1), (-1, 1), (1, -1), (1, 1), (2, -1), (2, 1), (0, 2), (-1, 2), (1, 2), (2, 2))
XP, XM, YP, YM = range(4)


def gather_project(side, x_hbm, g_ref, wq_hbm, wk_hbm, wv_hbm, q_ref, k_ref, v_ref, xbuf, tokens, wraw, wflat, stage,
                   in_sem, send_sem, pair_send_sem, link_sem, pair_sem):
    rows, depth = xbuf.shape
    half, quarter = rows // 2, rows // 4
    heads = wraw.shape[1] // depth
    cols = heads * LANES
    me = lax.axis_index("tp")
    core = lax.rem(me, CORES)
    chip = me // CORES
    my_x, my_y = lax.rem(chip, side), chip // side

    def chip_at(dx, dy):
        return lax.rem(my_y + dy + side, side) * side + lax.rem(my_x + dx + side, side)

    def device(chip_index, core_index):
        return {"tp": chip_index * CORES + core_index}

    neighbour = (chip_at(1, 0), chip_at(-1, 0), chip_at(0, 1), chip_at(0, -1))
    other = 1 - core

    copies_in = [pltpu.make_async_copy(x_hbm, xbuf, in_sem.at[0])]
    for i, w in enumerate((wq_hbm, wk_hbm, wv_hbm)):
        copies_in.append(pltpu.make_async_copy(w, wraw.at[i], in_sem.at[1 + i]))
    for copy in copies_in:
        copy.start()

    barrier = pltpu.get_barrier_semaphore()
    for chip_index in neighbour:
        pl.semaphore_signal(barrier, inc=1, device_id=device(chip_index, core), device_id_type=MESH)
    pl.semaphore_signal(barrier, inc=1, device_id=device(chip, other), device_id_type=MESH)

    def piece(dx, dy, is_q, part=None):
        start = chip_at(dx, dy) * (CORES * rows) + is_q * (CORES * half) + core * half
        if part is None:
            return tokens.at[pl.ds(pl.multiple_of(start, half), half)]
        return tokens.at[pl.ds(pl.multiple_of(start + part * quarter, quarter), quarter)]

    def link_copy(link, seq, ref):
        return pltpu.make_async_remote_copy(
            src_ref=ref, dst_ref=ref, send_sem=send_sem.at[link], recv_sem=link_sem.at[link, seq],
            device_id=device(neighbour[link], core), device_id_type=MESH)

    def pair_copy(step, is_q):
        dx, dy = ORDER[step]
        ref = piece(dy, dx, 1) if is_q else piece(dx, dy, 0)
        return pltpu.make_async_remote_copy(
            src_ref=ref, dst_ref=ref, send_sem=pair_send_sem.at[step % 4], recv_sem=pair_sem.at[step, is_q],
            device_id=device(chip, other), device_id_type=MESH)

    def send(link, seq):
        is_y = link >= YP
        back = -1 if link in (XP, YP) else 1
        part = 0 if link in (XP, YP) else 1
        lateral = {1: 0, 3: -1, 4: 1, 5: 2, 6: 0, 7: -1, 8: 1, 9: 2}
        if seq == 0:
            off, second, sub = (0, 0), 0, None
        elif seq == 2:
            off, second, sub = (back, 0), 0, part
        elif seq in (1, 3, 4, 5):
            off, second, sub = (0, lateral[seq]), 1, None
        else:
            off, second, sub = (back, lateral[seq]), 1, part
        if is_y:
            off = (off[1], off[0])
        link_copy(link, seq, piece(*off, second ^ int(is_y), sub)).start()

    def arrived(link, seq):
        n = quarter if seq in (2, 6, 7, 8, 9) else half
        link_copy(link, seq, tokens.at[pl.ds(0, n)]).wait_recv()

    links = (XP, XM, YP, YM)

    copies_in[0].wait()
    own = chip * (CORES * rows) + core * half
    norm_rows = 16

    def normalize(i, _):
        xf = xbuf[pl.ds(pl.multiple_of(i * norm_rows, norm_rows), norm_rows), :].astype(jnp.float32)
        mean_sq = jnp.mean(xf * xf, axis=-1, keepdims=True)
        n = (xf * lax.rsqrt(mean_sq + 1e-6) * g_ref[...]).astype(jnp.bfloat16)
        per_half = half // norm_rows
        dst = own + (i // per_half) * (CORES * half) + lax.rem(i, per_half) * norm_rows
        tokens[pl.ds(pl.multiple_of(dst, norm_rows), norm_rows), :] = n
        return 0

    lax.fori_loop(0, rows // norm_rows, normalize, 0)

    pl.semaphore_wait(barrier, 5)
    for seq in (0, 1):
        for link in links:
            send(link, seq)
        if seq == 0:
            pair_copy(0, 0).start()
            pair_copy(0, 1).start()

    wrows = stage.shape[1] // heads
    for i in range(3):
        copies_in[1 + i].wait()

        def relayout(j, _, i=i):
            src = pl.multiple_of(j * (wrows * heads), wrows * heads)
            dst = pl.multiple_of(j * wrows, wrows)
            stage[i] = wraw[i, pl.ds(src, wrows * heads), :].astype(jnp.float32)
            for h in range(heads):
                wflat[pl.ds(dst, wrows), pl.ds(i * cols + h * LANES, LANES)] = stage[i, pl.ds(h, wrows, stride=heads), :].astype(jnp.bfloat16)
            return 0

        lax.fori_loop(0, depth // wrows, relayout, 0)

    events = {
        1: ([(l, 0) for l in links], [(l, s) for s in (2, 3, 4) for l in links], (1, 2)),
        3: ([(l, 1) for l in links], [], (3, 4)),
        5: ([(l, 2) for l in links], [(l, s) for s in (5, 6) for l in links], (5,)),
        6: ([(l, 3) for l in links], [(l, 7) for l in links], (6, 7)),
        8: ([(l, 4) for l in links], [(l, 8) for l in links], (8, 9)),
        10: ([(l, 5) for l in links], [(l, 9) for l in links], (10, 11)),
        12: ([(l, 6) for l in links], [], (12,)),
        13: ([(l, 7) for l in links], [], (13,)),
        14: ([(l, 8) for l in links], [], (14,)),
        15: ([(l, 9) for l in links], [], (15,)),
    }

    def body(s, _):
        step, sub = s // 2, lax.rem(s, 2)
        for at, (waits, sends, pairs) in events.items():
            @pl.when(s == 2 * at)
            def _(waits=waits, sends=sends, pairs=pairs):
                for w in waits:
                    arrived(*w)
                for x in sends:
                    send(*x)
                for p in pairs:
                    pair_copy(p, 0).start()
                    pair_copy(p, 1).start()

        @pl.when(sub == 1)
        def _():
            for is_q in range(2):
                pltpu.make_async_remote_copy(
                    src_ref=tokens.at[pl.ds(0, half)], dst_ref=tokens.at[pl.ds(0, half)], send_sem=pair_send_sem.at[0],
                    recv_sem=pair_sem.at[step, is_q], device_id=device(chip, other), device_id_type=MESH).wait_recv()

        dx, dy = jnp.int32(0), jnp.int32(0)
        for k, (ox, oy) in enumerate(ORDER):
            dx = jnp.where(step == k, ox, dx)
            dy = jnp.where(step == k, oy, dy)
        plane = core + sub * (1 - 2 * core)
        chips = (chip_at(dx, dy), chip_at(dy, dx))
        src = [pl.multiple_of(chips[i] * (CORES * rows) + i * (CORES * half) + plane * half, half) for i in range(2)]
        dst = [pl.multiple_of(((chips[i] * CORES + plane) * rows + i * half) * heads, half * heads) for i in range(2)]
        lhs = jnp.concatenate([tokens[pl.ds(src[i], half), :] for i in range(2)], axis=0)
        for i, out in enumerate((q_ref, k_ref, v_ref)):
            for b in range(cols // 256):
                acc = jnp.dot(lhs, wflat[:, pl.ds(i * cols + b * 256, 256)], preferred_element_type=jnp.float32)
                for h in range(2):
                    stage[i, pl.ds(b * 2 + h, rows, stride=heads), :] = acc[:, h * LANES:(h + 1) * LANES]
            for j in range(2):
                out[pl.ds(dst[j], half * heads), :] = stage[i, pl.ds(j * half * heads, half * heads), :].astype(jnp.bfloat16)
        return 0

    lax.fori_loop(0, 2 * len(ORDER), body, 0)

    per_link = 5 * half + 5 * quarter
    for link in links:
        link_copy(link, 0, tokens.at[pl.ds(0, per_link)]).wait_send()
    for i in range(4):
        ref = tokens.at[pl.ds(0, 8 * half)]
        pltpu.make_async_remote_copy(
            src_ref=ref, dst_ref=ref, send_sem=pair_send_sem.at[i], recv_sem=pair_sem.at[0, 0],
            device_id=device(chip, other), device_id_type=MESH).wait_send()


def drain(pieces, *refs):
    ins, outs, sem = refs[:3], refs[3:6], refs[6]
    n = ins[0].shape[0] // pieces
    copies = [pltpu.make_async_copy(ins[i].at[pl.ds(p * n, n)], outs[i].at[pl.ds(p * n, n)], sem.at[i, p])
              for p in range(pieces) for i in range(3)]
    for copy in copies:
        copy.start()
    for copy in copies:
        copy.wait()


def solution(mesh):
    size = mesh.shape["tp"]
    side = math.isqrt(size // CORES)
    assert side * side * CORES == size and side * side == len(ORDER)

    def local_step(x, gain, wq, wk, wv):
        rows, depth = x.shape
        heads = wq.shape[1]
        total = rows * size
        flat = [w.reshape(depth * heads, LANES) for w in (wq, wk, wv)]
        vmem_out = pltpu.VMEM((total * heads, LANES), jnp.bfloat16)
        outs = pl.pallas_call(
            functools.partial(gather_project, side),
            out_shape=(vmem_out,) * 3,
            in_specs=[pl.BlockSpec(memory_space=pl.ANY), pl.BlockSpec(memory_space=pltpu.VMEM)] + [pl.BlockSpec(memory_space=pl.ANY)] * 3,
            out_specs=[pl.BlockSpec(memory_space=pltpu.VMEM)] * 3,
            scratch_shapes=[
                pltpu.VMEM((rows, depth), jnp.bfloat16),
                pltpu.VMEM((total, depth), jnp.bfloat16),
                pltpu.VMEM((3, depth * heads, LANES), jnp.bfloat16),
                pltpu.VMEM((depth, 3 * heads * LANES), jnp.bfloat16),
                pltpu.VMEM((3, rows * heads, LANES), jnp.float32),
                pltpu.SemaphoreType.DMA((4,)),
                pltpu.SemaphoreType.DMA((4,)),
                pltpu.SemaphoreType.DMA((4,)),
                pltpu.SemaphoreType.DMA((4, 10)),
                pltpu.SemaphoreType.DMA((len(ORDER), 2)),
            ],
            compiler_params=pltpu.CompilerParams(collective_id=0, has_side_effects=True, vmem_limit_bytes=36 * 1024 * 1024),
            name="gather_project",
        )(x, gain.reshape(1, depth), *flat)
        out = jax.ShapeDtypeStruct((total * heads, LANES), jnp.bfloat16)
        outs = pl.pallas_call(
            functools.partial(drain, 4),
            out_shape=(out,) * 3,
            in_specs=[pl.BlockSpec(memory_space=pltpu.VMEM)] * 3,
            out_specs=[pl.BlockSpec(memory_space=pl.ANY)] * 3,
            scratch_shapes=[pltpu.SemaphoreType.DMA((3, 4))],
            compiler_params=pltpu.CompilerParams(vmem_limit_bytes=1024 * 1024),
            name="drain",
        )(*outs)
        return tuple(o.reshape(total, heads, LANES) for o in outs)

    row_spec = P(("dp", "tp"), None)
    head_spec = P(None, "tp", None)
    out_spec = P("dp", "tp", None)
    return jax.shard_map(local_step, mesh=mesh, in_specs=(row_spec, P(None), head_spec, head_spec, head_spec),
                         out_specs=(out_spec, out_spec, out_spec), check_vma=False)
```

time: 247 us -> 68.4 us (0.28)
  local copies, waits for them, and re-layouts: 120 us -> 0 us
  waiting for transfers between devices: 71.7 us -> 0 us
  Pallas kernels: 0 us -> 67.6 us
  matrix products: 37.6 us -> 0 us
  between operations: 14.1 us -> 0.64 us
  other arithmetic: 3.34 us -> 0 us
    unnamed x11 -> x0, local copies, waits for them, and re-layouts: 120 us -> none
    all_gather x1 -> x0, waiting for transfers between devices: 71.7 us -> none  [local_step(): gathered = lax.all_gather(normed, 'tp', axis=0, tiled=True)]
    pallas_call x0 -> x2, Pallas kernels: none -> 67.6 us  [the longest x1 59.1 us: local_step(): pl.pallas_call(functools.partial(gather_project, side), out_shape=(vmem_o...]
    dot_general x3 -> x0, matrix products: 37.6 us -> none  [the longest x1 12.6 us: local_step(): jnp.einsum('td,dhk->thk', gathered, wv_local, preferred_element_type=jnp....]
  transfers between devices with their start and end apart: 1 -> 0, of which waited for: 1 -> 0; matrix products, arithmetic and copies ran while one was open for 0% -> 0% of each run, Pallas kernels for 0% -> 0%
where the time goes in v1:
time: 68.4 us; the launch traced here: 68.2 us
  Pallas kernels  67.6 us (99%)
    pallas_call x1, Pallas kernels, local_step(): pl.pallas_call(functools.partial(gather_project, side), out_shape=(vmem_o...  59.1 us
    pallas_call x1, Pallas kernels, local_step(): pl.pallas_call(functools.partial(drain, 4), out_shape=(out,) * 3, in_spec...  8.48 us

profile of v1, /device:TPU:97, one launch (start us, length us, event | category | flops | bytes accessed | tf_op | source)
XLA Modules:
  0.0 68.2 jit_solution(4993873859485544953)
XLA Ops:
  0.6 59.1 %gather_project.1 = (bf16[32768,128]{1,0:T(8,128)(2,1)S(1)}, bf16[32768,128]{1,0:T(8,128)(2,1)S(1)}, bf16[32768,128]{1,0:T(8,128)(2,1)S(1)}) custom-call(bf16[256,1024]{1,0:T(8,128)(2,1)} %x_hbm.1, f32[1,1024]{1,0:T(1,128)} %bitcast.10, bf16[4096,128]{1,0:T(8,128)(2,1)} %bitcast.7, bf16[4096,128]{1,0:T(8,128)(2,1)} %bitcast.8, bf16[4096,128]{1,0:T(8,128)(2,1)} %bitcast.9), custom_call_target="tpu_custom_call" | custom-call | tf_op jit(solution)/shard_map/gather_project/pallas_call | solution.py:213
  59.8 8.5 %drain.1 = (bf16[32768,128]{1,0:T(8,128)(2,1)}, bf16[32768,128]{1,0:T(8,128)(2,1)}, bf16[32768,128]{1,0:T(8,128)(2,1)}) custom-call(bf16[32768,128]{1,0:T(8,128)(2,1)S(1)} %get-tuple-element.9.refs_0_, bf16[32768,128]{1,0:T(8,128)(2,1)S(1)} %get-tuple-element.10.refs_1_, bf16[32768,128]{1,0:T(8,128)(2,1)S(1)} %get-tuple-element.11.refs_2_), custom_call_target="tpu_custom_call" | custom-call | tf_op jit(solution)/shard_map/drain/pallas_call | solution.py:234

commit v2 on v1

--- a/solution.py
+++ b/solution.py
@@ -16,7 +16,36 @@
 XP, XM, YP, YM = range(4)
 
 
-def gather_project(side, x_hbm, g_ref, wq_hbm, wk_hbm, wv_hbm, q_ref, k_ref, v_ref, xbuf, tokens, wraw, wflat, stage,
+TAIL = 2
+VMEM_LIMIT = 63438848 - 28311552 - TAIL * 1048576
+
+
+def places(side, rows, heads, chip_at, step, plane):
+    half = rows // 2
+    dx, dy = jnp.int32(0), jnp.int32(0)
+    for k, (ox, oy) in enumerate(ORDER):
+        dx = jnp.where(step == k, ox, dx)
+        dy = jnp.where(step == k, oy, dy)
+    chips = (chip_at(dx, dy), chip_at(dy, dx))
+    src = [pl.multiple_of(chips[i] * (CORES * rows) + i * (CORES * half) + plane * half, half) for i in range(2)]
+    dst = [pl.multiple_of(((chips[i] * CORES + plane) * rows + i * half) * heads, half * heads) for i in range(2)]
+    return src, dst
+
+
+def project(tokens, wflat, stage, src, half, outs):
+    lhs = jnp.concatenate([tokens[pl.ds(r, half), :] for r in src], axis=0)
+    heads = wflat.shape[1] // (3 * LANES)
+    cols = heads * LANES
+    for i, (out, dst) in enumerate(outs):
+        for b in range(cols // 256):
+            acc = jnp.dot(lhs, wflat[:, pl.ds(i * cols + b * 256, 256)], preferred_element_type=jnp.float32)
+            for h in range(2):
+                stage[i, pl.ds(b * 2 + h, 2 * half, stride=heads), :] = acc[:, h * LANES:(h + 1) * LANES]
+        for j in range(2):
+            out[pl.ds(dst[j], half * heads), :] = stage[i, pl.ds(j * half * heads, half * heads), :].astype(jnp.bfloat16)
+
+
+def gather_project(side, x_hbm, g_ref, wq_hbm, wk_hbm, wv_hbm, q_ref, k_ref, v_ref, last, wflat, xbuf, tokens, wraw, stage,
                    in_sem, send_sem, pair_send_sem, link_sem, pair_sem):
     rows, depth = xbuf.shape
     half, quarter = rows // 2, rows // 4
@@ -53,14 +82,23 @@
             return tokens.at[pl.ds(pl.multiple_of(start, half), half)]
         return tokens.at[pl.ds(pl.multiple_of(start + part * quarter, quarter), quarter)]
 
-    def link_copy(link, seq, ref):
+    def last_piece(step, is_q, part=None):
+        start = ((step - len(ORDER) + TAIL) * 2 + is_q) * (CORES * half) + core * half
+        if part is None:
+            return last.at[pl.ds(pl.multiple_of(start, half), half)]
+        return last.at[pl.ds(pl.multiple_of(start + part * quarter, quarter), quarter)]
+
+    def link_copy(link, seq, ref, dst=None):
         return pltpu.make_async_remote_copy(
-            src_ref=ref, dst_ref=ref, send_sem=send_sem.at[link], recv_sem=link_sem.at[link, seq],
+            src_ref=ref, dst_ref=ref if dst is None else dst, send_sem=send_sem.at[link], recv_sem=link_sem.at[link, seq],
             device_id=device(neighbour[link], core), device_id_type=MESH)
 
     def pair_copy(step, is_q):
         dx, dy = ORDER[step]
-        ref = piece(dy, dx, 1) if is_q else piece(dx, dy, 0)
+        if step >= len(ORDER) - TAIL:
+            ref = last_piece(step, is_q)
+        else:
+            ref = piece(dy, dx, 1) if is_q else piece(dx, dy, 0)
         return pltpu.make_async_remote_copy(
             src_ref=ref, dst_ref=ref, send_sem=pair_send_sem.at[step % 4], recv_sem=pair_sem.at[step, is_q],
             device_id=device(chip, other), device_id_type=MESH)
@@ -80,7 +118,9 @@
             off, second, sub = (back, lateral[seq]), 1, part
         if is_y:
             off = (off[1], off[0])
-        link_copy(link, seq, piece(*off, second ^ int(is_y), sub)).start()
+        step = len(ORDER) - 10 + seq
+        dst = last_piece(step, 1 - int(is_y), sub) if step >= len(ORDER) - TAIL else None
+        link_copy(link, seq, piece(*off, second ^ int(is_y), sub), dst).start()
 
     def arrived(link, seq):
         n = quarter if seq in (2, 6, 7, 8, 9) else half
@@ -158,22 +198,10 @@
                     src_ref=tokens.at[pl.ds(0, half)], dst_ref=tokens.at[pl.ds(0, half)], send_sem=pair_send_sem.at[0],
                     recv_sem=pair_sem.at[step, is_q], device_id=device(chip, other), device_id_type=MESH).wait_recv()
 
-        dx, dy = jnp.int32(0), jnp.int32(0)
-        for k, (ox, oy) in enumerate(ORDER):
-            dx = jnp.where(step == k, ox, dx)
-            dy = jnp.where(step == k, oy, dy)
-        plane = core + sub * (1 - 2 * core)
-        chips = (chip_at(dx, dy), chip_at(dy, dx))
-        src = [pl.multiple_of(chips[i] * (CORES * rows) + i * (CORES * half) + plane * half, half) for i in range(2)]
-        dst = [pl.multiple_of(((chips[i] * CORES + plane) * rows + i * half) * heads, half * heads) for i in range(2)]
-        lhs = jnp.concatenate([tokens[pl.ds(src[i], half), :] for i in range(2)], axis=0)
-        for i, out in enumerate((q_ref, k_ref, v_ref)):
-            for b in range(cols // 256):
-                acc = jnp.dot(lhs, wflat[:, pl.ds(i * cols + b * 256, 256)], preferred_element_type=jnp.float32)
-                for h in range(2):
-                    stage[i, pl.ds(b * 2 + h, rows, stride=heads), :] = acc[:, h * LANES:(h + 1) * LANES]
-            for j in range(2):
-                out[pl.ds(dst[j], half * heads), :] = stage[i, pl.ds(j * half * heads, half * heads), :].astype(jnp.bfloat16)
+        @pl.when(step < len(ORDER) - TAIL)
+        def _():
+            src, dst = places(side, rows, heads, chip_at, step, core + sub * (1 - 2 * core))
+            project(tokens, wflat, stage, src, half, ((q_ref, dst), (k_ref, dst), (v_ref, dst)))
         return 0
 
     lax.fori_loop(0, 2 * len(ORDER), body, 0)
@@ -188,15 +216,48 @@
             device_id=device(chip, other), device_id_type=MESH).wait_send()
 
 
-def drain(pieces, *refs):
-    ins, outs, sem = refs[:3], refs[3:6], refs[6]
-    n = ins[0].shape[0] // pieces
-    copies = [pltpu.make_async_copy(ins[i].at[pl.ds(p * n, n)], outs[i].at[pl.ds(p * n, n)], sem.at[i, p])
-              for p in range(pieces) for i in range(3)]
-    for copy in copies:
-        copy.start()
-    for copy in copies:
-        copy.wait()
+def drain(side, rows, q_in, k_in, v_in, last, wflat, q_out, k_out, v_out, tail, stage, main_sem, tail_sem):
+    ins, outs = (q_in, k_in, v_in), (q_out, k_out, v_out)
+    half = rows // 2
+    heads = wflat.shape[1] // (3 * LANES)
+    chip = lax.axis_index("tp") // CORES
+    my_x, my_y = lax.rem(chip, side), chip // side
+
+    def chip_at(dx, dy):
+        return lax.rem(my_y + dy + side, side) * side + lax.rem(my_x + dx + side, side)
+
+    first = len(ORDER) - TAIL
+    for dx, dy in ORDER:
+        has = (ORDER.index((dx, dy)) < first, ORDER.index((dy, dx)) < first)
+        base = chip_at(dx, dy) * (CORES * rows)
+        if has[0] and has[1]:
+            parts = [(0, CORES * rows)]
+        else:
+            parts = [(c * rows + h * half, half) for c in range(CORES) for h in range(2) if has[h]]
+        for off, n in parts:
+            at = pl.ds(pl.multiple_of((base + off) * heads, half * heads), n * heads)
+            for i in range(3):
+                pltpu.make_async_copy(ins[i].at[at], outs[i].at[at], main_sem.at[i]).start()
+
+    step_rows = 2 * half * heads
+
+    def body(s, _):
+        step, plane = first + s // 2, lax.rem(s, 2)
+        dst = places(side, rows, heads, chip_at, step, plane)[1]
+        src = [pl.multiple_of(((s // 2) * 2 + j) * (CORES * half) + plane * half, half) for j in range(2)]
+        mine = [pl.multiple_of(s * step_rows + j * half * heads, half * heads) for j in range(2)]
+        project(last, wflat, stage, src, half, tuple((tail.at[i], mine) for i in range(3)))
+        for i in range(3):
+            for j in range(2):
+                pltpu.make_async_copy(tail.at[i, pl.ds(mine[j], half * heads)], outs[i].at[pl.ds(dst[j], half * heads)], tail_sem.at[i]).start()
+        return 0
+
+    lax.fori_loop(0, 2 * TAIL, body, 0)
+    for i in range(3):
+        n = first * CORES * step_rows
+        pltpu.make_async_copy(ins[i].at[pl.ds(0, n)], outs[i].at[pl.ds(0, n)], main_sem.at[i]).wait()
+        n = TAIL * CORES * step_rows
+        pltpu.make_async_copy(tail.at[i], outs[i].at[pl.ds(0, n)], tail_sem.at[i]).wait()
 
 
 def solution(mesh):
@@ -212,14 +273,13 @@
         vmem_out = pltpu.VMEM((total * heads, LANES), jnp.bfloat16)
         outs = pl.pallas_call(
             functools.partial(gather_project, side),
-            out_shape=(vmem_out,) * 3,
+            out_shape=(vmem_out,) * 3 + (pltpu.VMEM((TAIL * CORES * rows, depth), jnp.bfloat16), pltpu.VMEM((depth, 3 * heads * LANES), jnp.bfloat16)),
             in_specs=[pl.BlockSpec(memory_space=pl.ANY), pl.BlockSpec(memory_space=pltpu.VMEM)] + [pl.BlockSpec(memory_space=pl.ANY)] * 3,
-            out_specs=[pl.BlockSpec(memory_space=pltpu.VMEM)] * 3,
+            out_specs=[pl.BlockSpec(memory_space=pltpu.VMEM)] * 5,
             scratch_shapes=[
                 pltpu.VMEM((rows, depth), jnp.bfloat16),
                 pltpu.VMEM((total, depth), jnp.bfloat16),
                 pltpu.VMEM((3, depth * heads, LANES), jnp.bfloat16),
-                pltpu.VMEM((depth, 3 * heads * LANES), jnp.bfloat16),
                 pltpu.VMEM((3, rows * heads, LANES), jnp.float32),
                 pltpu.SemaphoreType.DMA((4,)),
                 pltpu.SemaphoreType.DMA((4,)),
@@ -227,17 +287,22 @@
                 pltpu.SemaphoreType.DMA((4, 10)),
                 pltpu.SemaphoreType.DMA((len(ORDER), 2)),
             ],
-            compiler_params=pltpu.CompilerParams(collective_id=0, has_side_effects=True, vmem_limit_bytes=36 * 1024 * 1024),
+            compiler_params=pltpu.CompilerParams(collective_id=0, has_side_effects=True, vmem_limit_bytes=50 * 1024 * 1024 // 2),
             name="gather_project",
         )(x, gain.reshape(1, depth), *flat)
         out = jax.ShapeDtypeStruct((total * heads, LANES), jnp.bfloat16)
         outs = pl.pallas_call(
-            functools.partial(drain, 4),
+            functools.partial(drain, side, rows),
             out_shape=(out,) * 3,
-            in_specs=[pl.BlockSpec(memory_space=pltpu.VMEM)] * 3,
+            in_specs=[pl.BlockSpec(memory_space=pltpu.VMEM)] * 5,
             out_specs=[pl.BlockSpec(memory_space=pl.ANY)] * 3,
-            scratch_shapes=[pltpu.SemaphoreType.DMA((3, 4))],
-            compiler_params=pltpu.CompilerParams(vmem_limit_bytes=1024 * 1024),
+            scratch_shapes=[
+                pltpu.VMEM((3, TAIL * CORES * rows * heads, LANES), jnp.bfloat16),
+                pltpu.VMEM((3, rows * heads, LANES), jnp.float32),
+                pltpu.SemaphoreType.DMA((3,)),
+                pltpu.SemaphoreType.DMA((3,)),
+            ],
+            compiler_params=pltpu.CompilerParams(vmem_limit_bytes=48 * 1024 * 1024 // 2),
             name="drain",
         )(*outs)
         return tuple(o.reshape(total, heads, LANES) for o in outs)

time: 68.4 us -> 66.1 us (0.966)
  Pallas kernels: 67.6 us -> 65.3 us
    pallas_call x1, Pallas kernels: 59.1 us -> 57 us  [local_step(): pl.pallas_call(functools.partial(gather_project, side), out_shape=(vmem_o...]
where the time goes in v2:
time: 66.1 us; the launch traced here: 65.9 us
  Pallas kernels  65.3 us (99%)
    pallas_call x1, Pallas kernels, local_step(): pl.pallas_call(functools.partial(gather_project, side), out_shape=(vmem_o...  57 us
    pallas_call x1, Pallas kernels, local_step(): pl.pallas_call(functools.partial(drain, side, rows), out_shape=(out,) * 3...  8.35 us

profile of v2, /device:TPU:97, one launch (start us, length us, event | category | flops | bytes accessed | tf_op | source)
XLA Modules:
  0.0 65.9 jit_solution(7908368560185171220)
XLA Ops:
  0.6 57.0 %gather_project.1 = (bf16[32768,128]{1,0:T(8,128)(2,1)S(1)}, bf16[32768,128]{1,0:T(8,128)(2,1)S(1)}, bf16[32768,128]{1,0:T(8,128)(2,1)S(1)}, bf16[1024,1024]{1,0:T(8,128)(2,1)S(1)}, bf16[1024,1536]{1,0:T(8,128)(2,1)S(1)}) custom-call(bf16[256,1024]{1,0:T(8,128)(2,1)} %x_hbm.1, f32[1,1024]{1,0:T(1,128)} %bitcast.10, bf16[4096,128]{1,0:T(8,128)(2,1)} %bitcast.7, ...), custom_call_target="tpu_custom_call" | custom-call | tf_op jit(solution)/shard_map/gather_project/pallas_call | solution.py:274
  57.6 8.4 %drain.1 = (bf16[32768,128]{1,0:T(8,128)(2,1)}, bf16[32768,128]{1,0:T(8,128)(2,1)}, bf16[32768,128]{1,0:T(8,128)(2,1)}) custom-call(bf16[32768,128]{1,0:T(8,128)(2,1)S(1)} %get-tuple-element.11.q_in, bf16[32768,128]{1,0:T(8,128)(2,1)S(1)} %get-tuple-element.12.k_in, bf16[32768,128]{1,0:T(8,128)(2,1)S(1)} %get-tuple-element.13.v_in, ...), custom_call_target="tpu_custom_call" | custom-call | tf_op jit(solution)/shard_map/drain/pallas_call | solution.py:294

commit v3 on v2

--- a/solution.py
+++ b/solution.py
@@ -45,7 +45,7 @@
             out[pl.ds(dst[j], half * heads), :] = stage[i, pl.ds(j * half * heads, half * heads), :].astype(jnp.bfloat16)
 
 
-def gather_project(side, x_hbm, g_ref, wq_hbm, wk_hbm, wv_hbm, q_ref, k_ref, v_ref, last, wflat, xbuf, tokens, wraw, stage,
+def gather_project(side, x_hbm, g_hbm, wq_hbm, wk_hbm, wv_hbm, q_ref, k_ref, v_ref, last, wflat, xbuf, g_ref, tokens, wraw, stage,
                    in_sem, send_sem, pair_send_sem, link_sem, pair_sem):
     rows, depth = xbuf.shape
     half, quarter = rows // 2, rows // 4
@@ -65,16 +65,17 @@
     neighbour = (chip_at(1, 0), chip_at(-1, 0), chip_at(0, 1), chip_at(0, -1))
     other = 1 - core
 
-    copies_in = [pltpu.make_async_copy(x_hbm, xbuf, in_sem.at[0])]
-    for i, w in enumerate((wq_hbm, wk_hbm, wv_hbm)):
-        copies_in.append(pltpu.make_async_copy(w, wraw.at[i], in_sem.at[1 + i]))
-    for copy in copies_in:
-        copy.start()
-
     barrier = pltpu.get_barrier_semaphore()
     for chip_index in neighbour:
         pl.semaphore_signal(barrier, inc=1, device_id=device(chip_index, core), device_id_type=MESH)
     pl.semaphore_signal(barrier, inc=1, device_id=device(chip, other), device_id_type=MESH)
+
+    halves_in = [pltpu.make_async_copy(x_hbm.at[pl.ds(h * half, half)], xbuf.at[pl.ds(h * half, half)], in_sem.at[h]) for h in range(2)]
+    gain_in = pltpu.make_async_copy(g_hbm, g_ref, in_sem.at[2])
+    weights_in = [pltpu.make_async_copy(w, wraw.at[i], in_sem.at[3 + i]) for i, w in enumerate((wq_hbm, wk_hbm, wv_hbm))]
+    halves_in[0].start()
+    gain_in.start()
+    halves_in[1].start()
 
     def piece(dx, dy, is_q, part=None):
         start = chip_at(dx, dy) * (CORES * rows) + is_q * (CORES * half) + core * half
@@ -128,32 +129,30 @@
 
     links = (XP, XM, YP, YM)
 
-    copies_in[0].wait()
     own = chip * (CORES * rows) + core * half
-    norm_rows = 16
-
-    def normalize(i, _):
-        xf = xbuf[pl.ds(pl.multiple_of(i * norm_rows, norm_rows), norm_rows), :].astype(jnp.float32)
-        mean_sq = jnp.mean(xf * xf, axis=-1, keepdims=True)
-        n = (xf * lax.rsqrt(mean_sq + 1e-6) * g_ref[...]).astype(jnp.bfloat16)
-        per_half = half // norm_rows
-        dst = own + (i // per_half) * (CORES * half) + lax.rem(i, per_half) * norm_rows
-        tokens[pl.ds(pl.multiple_of(dst, norm_rows), norm_rows), :] = n
-        return 0
-
-    lax.fori_loop(0, rows // norm_rows, normalize, 0)
-
-    pl.semaphore_wait(barrier, 5)
-    for seq in (0, 1):
-        for link in links:
-            send(link, seq)
-        if seq == 0:
-            pair_copy(0, 0).start()
-            pair_copy(0, 1).start()
+    norm_rows = 32
+    gain_in.wait()
+    for h in range(2):
+        halves_in[h].wait()
+        if h == 0:
+            for copy in weights_in:
+                copy.start()
+        for r in range(0, half, norm_rows):
+            xf = xbuf[pl.ds(h * half + r, norm_rows), :].astype(jnp.float32)
+            mean_sq = jnp.mean(xf * xf, axis=-1, keepdims=True)
+            n = (xf * lax.rsqrt(mean_sq + 1e-6) * g_ref[...]).astype(jnp.bfloat16)
+            tokens[pl.ds(pl.multiple_of(own + h * (CORES * half) + r, norm_rows), norm_rows), :] = n
+        if h == 0:
+            pl.semaphore_wait(barrier, 5)
+        for link in (links[:2] if h == 0 else links[2:]):
+            send(link, 0)
+        pair_copy(0, h).start()
+    for link in links:
+        send(link, 1)
 
     wrows = stage.shape[1] // heads
     for i in range(3):
-        copies_in[1 + i].wait()
+        weights_in[i].wait()
 
         def relayout(j, _, i=i):
             src = pl.multiple_of(j * (wrows * heads), wrows * heads)
@@ -178,6 +177,18 @@
         15: ([(l, 9) for l in links], [], (15,)),
     }
 
+    def project_piece(step, plane):
+        src, dst = places(side, rows, heads, chip_at, step, plane)
+        project(tokens, wflat, stage, src, half, ((q_ref, dst), (k_ref, dst), (v_ref, dst)))
+
+    def pair_arrived(step):
+        for is_q in range(2):
+            pltpu.make_async_remote_copy(
+                src_ref=tokens.at[pl.ds(0, half)], dst_ref=tokens.at[pl.ds(0, half)], send_sem=pair_send_sem.at[0],
+                recv_sem=pair_sem.at[step, is_q], device_id=device(chip, other), device_id_type=MESH).wait_recv()
+
+    first = len(ORDER) - TAIL
+
     def body(s, _):
         step, sub = s // 2, lax.rem(s, 2)
         for at, (waits, sends, pairs) in events.items():
@@ -191,20 +202,17 @@
                     pair_copy(p, 0).start()
                     pair_copy(p, 1).start()
 
-        @pl.when(sub == 1)
+        @pl.when(jnp.logical_and(sub == 1, step > 0))
         def _():
-            for is_q in range(2):
-                pltpu.make_async_remote_copy(
-                    src_ref=tokens.at[pl.ds(0, half)], dst_ref=tokens.at[pl.ds(0, half)], send_sem=pair_send_sem.at[0],
-                    recv_sem=pair_sem.at[step, is_q], device_id=device(chip, other), device_id_type=MESH).wait_recv()
-
-        @pl.when(step < len(ORDER) - TAIL)
+            pair_arrived(step - 1)
+
+        @pl.when(jnp.where(sub == 0, step < first, jnp.logical_and(step > 0, step <= first)))
         def _():
-            src, dst = places(side, rows, heads, chip_at, step, core + sub * (1 - 2 * core))
-            project(tokens, wflat, stage, src, half, ((q_ref, dst), (k_ref, dst), (v_ref, dst)))
+            project_piece(step - sub, core + sub * (1 - 2 * core))
         return 0
 
     lax.fori_loop(0, 2 * len(ORDER), body, 0)
+    pair_arrived(len(ORDER) - 1)
 
     per_link = 5 * half + 5 * quarter
     for link in links:
@@ -274,14 +282,15 @@
         outs = pl.pallas_call(
             functools.partial(gather_project, side),
             out_shape=(vmem_out,) * 3 + (pltpu.VMEM((TAIL * CORES * rows, depth), jnp.bfloat16), pltpu.VMEM((depth, 3 * heads * LANES), jnp.bfloat16)),
-            in_specs=[pl.BlockSpec(memory_space=pl.ANY), pl.BlockSpec(memory_space=pltpu.VMEM)] + [pl.BlockSpec(memory_space=pl.ANY)] * 3,
+            in_specs=[pl.BlockSpec(memory_space=pltpu.HBM)] * 5,
             out_specs=[pl.BlockSpec(memory_space=pltpu.VMEM)] * 5,
             scratch_shapes=[
                 pltpu.VMEM((rows, depth), jnp.bfloat16),
+                pltpu.VMEM((1, depth), jnp.float32),
                 pltpu.VMEM((total, depth), jnp.bfloat16),
                 pltpu.VMEM((3, depth * heads, LANES), jnp.bfloat16),
                 pltpu.VMEM((3, rows * heads, LANES), jnp.float32),
-                pltpu.SemaphoreType.DMA((4,)),
+                pltpu.SemaphoreType.DMA((6,)),
                 pltpu.SemaphoreType.DMA((4,)),
                 pltpu.SemaphoreType.DMA((4,)),
                 pltpu.SemaphoreType.DMA((4, 10)),

time: 66.1 us -> 64 us (0.968)
  Pallas kernels: 65.3 us -> 63.3 us
    pallas_call x1, Pallas kernels: 57 us -> 54.9 us  [local_step(): pl.pallas_call(functools.partial(gather_project, side), out_shape=(vmem_o...]
where the time goes in v3:
time: 64 us; the launch traced here: 63.9 us
  Pallas kernels  63.3 us (99%)
  between operations  0.64 us (1%)
    pallas_call x1, Pallas kernels, local_step(): pl.pallas_call(functools.partial(gather_project, side), out_shape=(vmem_o...  54.9 us
    pallas_call x1, Pallas kernels, local_step(): pl.pallas_call(functools.partial(drain, side, rows), out_shape=(out,) * 3...  8.35 us

profile of v3, /device:TPU:97, one launch (start us, length us, event | category | flops | bytes accessed | tf_op | source)
XLA Modules:
  0.0 63.9 jit_solution(6428223112746245930)
XLA Ops:
  0.6 54.9 %gather_project.1 = (bf16[32768,128]{1,0:T(8,128)(2,1)S(1)}, bf16[32768,128]{1,0:T(8,128)(2,1)S(1)}, bf16[32768,128]{1,0:T(8,128)(2,1)S(1)}, bf16[1024,1024]{1,0:T(8,128)(2,1)S(1)}, bf16[1024,1536]{1,0:T(8,128)(2,1)S(1)}) custom-call(bf16[256,1024]{1,0:T(8,128)(2,1)} %x_hbm.1, f32[1,1024]{1,0:T(1,128)} %bitcast.10, bf16[4096,128]{1,0:T(8,128)(2,1)} %bitcast.7, ...), custom_call_target="tpu_custom_call" | custom-call | tf_op jit(solution)/shard_map/gather_project/pallas_call | solution.py:282
  55.6 8.4 %drain.1 = (bf16[32768,128]{1,0:T(8,128)(2,1)}, bf16[32768,128]{1,0:T(8,128)(2,1)}, bf16[32768,128]{1,0:T(8,128)(2,1)}) custom-call(bf16[32768,128]{1,0:T(8,128)(2,1)S(1)} %get-tuple-element.11.q_in, bf16[32768,128]{1,0:T(8,128)(2,1)S(1)} %get-tuple-element.12.k_in, bf16[32768,128]{1,0:T(8,128)(2,1)S(1)} %get-tuple-element.13.v_in, ...), custom_call_target="tpu_custom_call" | custom-call | tf_op jit(solution)/shard_map/drain/pallas_call | solution.py:303

commit v4 on v3

--- a/solution.py
+++ b/solution.py
@@ -46,9 +46,9 @@
 
 
 def gather_project(side, x_hbm, g_hbm, wq_hbm, wk_hbm, wv_hbm, q_ref, k_ref, v_ref, last, wflat, xbuf, g_ref, tokens, wraw, stage,
-                   in_sem, send_sem, pair_send_sem, link_sem, pair_sem):
+                   in_sem, send_sem, link_sem, pair_sem):
     rows, depth = xbuf.shape
-    half, quarter = rows // 2, rows // 4
+    half, quarter, eighth = rows // 2, rows // 4, rows // 8
     heads = wraw.shape[1] // depth
     cols = heads * LANES
     me = lax.axis_index("tp")
@@ -72,43 +72,50 @@
 
     halves_in = [pltpu.make_async_copy(x_hbm.at[pl.ds(h * half, half)], xbuf.at[pl.ds(h * half, half)], in_sem.at[h]) for h in range(2)]
     gain_in = pltpu.make_async_copy(g_hbm, g_ref, in_sem.at[2])
-    weights_in = [pltpu.make_async_copy(w, wraw.at[i], in_sem.at[3 + i]) for i, w in enumerate((wq_hbm, wk_hbm, wv_hbm))]
+    weights_in = [pltpu.make_async_copy(w, wraw.at[i], in_sem.at[3]) for i, w in enumerate((wq_hbm, wk_hbm, wv_hbm))]
     halves_in[0].start()
     gain_in.start()
     halves_in[1].start()
 
-    def piece(dx, dy, is_q, part=None):
+    def piece(dx, dy, is_q, part=None, sub=None):
         start = chip_at(dx, dy) * (CORES * rows) + is_q * (CORES * half) + core * half
         if part is None:
             return tokens.at[pl.ds(pl.multiple_of(start, half), half)]
-        return tokens.at[pl.ds(pl.multiple_of(start + part * quarter, quarter), quarter)]
-
-    def last_piece(step, is_q, part=None):
+        if sub is None:
+            return tokens.at[pl.ds(pl.multiple_of(start + part * quarter, quarter), quarter)]
+        return tokens.at[pl.ds(pl.multiple_of(start + part * quarter + sub * eighth, eighth), eighth)]
+
+    def last_piece(step, is_q, part=None, sub=None):
         start = ((step - len(ORDER) + TAIL) * 2 + is_q) * (CORES * half) + core * half
         if part is None:
             return last.at[pl.ds(pl.multiple_of(start, half), half)]
-        return last.at[pl.ds(pl.multiple_of(start + part * quarter, quarter), quarter)]
+        if sub is None:
+            return last.at[pl.ds(pl.multiple_of(start + part * quarter, quarter), quarter)]
+        return last.at[pl.ds(pl.multiple_of(start + part * quarter + sub * eighth, eighth), eighth)]
 
     def link_copy(link, seq, ref, dst=None):
         return pltpu.make_async_remote_copy(
-            src_ref=ref, dst_ref=ref if dst is None else dst, send_sem=send_sem.at[link], recv_sem=link_sem.at[link, seq],
+            src_ref=ref, dst_ref=ref if dst is None else dst, send_sem=send_sem, recv_sem=link_sem.at[seq],
             device_id=device(neighbour[link], core), device_id_type=MESH)
 
-    def pair_copy(step, is_q):
+    def to_pair(ref, sem):
+        return pltpu.make_async_remote_copy(
+            src_ref=ref, dst_ref=ref, send_sem=send_sem, recv_sem=pair_sem.at[sem],
+            device_id=device(chip, other), device_id_type=MESH)
+
+    def pair_copies(step):
         dx, dy = ORDER[step]
         if step >= len(ORDER) - TAIL:
-            ref = last_piece(step, is_q)
+            refs = [last_piece(step, 0), last_piece(step, 1)]
         else:
-            ref = piece(dy, dx, 1) if is_q else piece(dx, dy, 0)
-        return pltpu.make_async_remote_copy(
-            src_ref=ref, dst_ref=ref, send_sem=pair_send_sem.at[step % 4], recv_sem=pair_sem.at[step, is_q],
-            device_id=device(chip, other), device_id_type=MESH)
+            refs = [piece(dx, dy, 0), piece(dy, dx, 1)]
+        return [(ref, step) for ref in refs]
 
     def send(link, seq):
         is_y = link >= YP
         back = -1 if link in (XP, YP) else 1
         part = 0 if link in (XP, YP) else 1
-        lateral = {1: 0, 3: -1, 4: 1, 5: 2, 6: 0, 7: -1, 8: 1, 9: 2}
+        lateral = {1: 0, 3: -1, 4: 1, 5: 2, 6: 0, 7: -1, 8: 1, 9: 2, 10: 2}
         if seq == 0:
             off, second, sub = (0, 0), 0, None
         elif seq == 2:
@@ -119,13 +126,19 @@
             off, second, sub = (back, lateral[seq]), 1, part
         if is_y:
             off = (off[1], off[0])
-        step = len(ORDER) - 10 + seq
-        dst = last_piece(step, 1 - int(is_y), sub) if step >= len(ORDER) - TAIL else None
-        link_copy(link, seq, piece(*off, second ^ int(is_y), sub), dst).start()
-
-    def arrived(link, seq):
-        n = quarter if seq in (2, 6, 7, 8, 9) else half
-        link_copy(link, seq, tokens.at[pl.ds(0, n)]).wait_recv()
+        second = second ^ int(is_y)
+        step = len(ORDER) - 10 + min(seq, 9)
+        if seq >= 9:
+            src = piece(*off, second, sub, seq - 9)
+            dst = last_piece(step, second, sub, seq - 9)
+        else:
+            src = piece(*off, second, sub)
+            dst = last_piece(step, second, sub) if step >= len(ORDER) - TAIL else None
+        link_copy(link, seq, src, dst).start()
+
+    def arrived(seq):
+        n = 4 * (eighth if seq >= 9 else quarter if seq in (2, 6, 7, 8) else half)
+        link_copy(XP, seq, tokens.at[pl.ds(0, n)]).wait_recv()
 
     links = (XP, XM, YP, YM)
 
@@ -146,13 +159,13 @@
             pl.semaphore_wait(barrier, 5)
         for link in (links[:2] if h == 0 else links[2:]):
             send(link, 0)
-        pair_copy(0, h).start()
+        to_pair(*pair_copies(0)[h]).start()
     for link in links:
         send(link, 1)
 
     wrows = stage.shape[1] // heads
+    pltpu.make_async_copy(wraw, wraw, in_sem.at[3]).wait()
     for i in range(3):
-        weights_in[i].wait()
 
         def relayout(j, _, i=i):
             src = pl.multiple_of(j * (wrows * heads), wrows * heads)
@@ -165,16 +178,15 @@
         lax.fori_loop(0, depth // wrows, relayout, 0)
 
     events = {
-        1: ([(l, 0) for l in links], [(l, s) for s in (2, 3, 4) for l in links], (1, 2)),
-        3: ([(l, 1) for l in links], [], (3, 4)),
-        5: ([(l, 2) for l in links], [(l, s) for s in (5, 6) for l in links], (5,)),
-        6: ([(l, 3) for l in links], [(l, 7) for l in links], (6, 7)),
-        8: ([(l, 4) for l in links], [(l, 8) for l in links], (8, 9)),
-        10: ([(l, 5) for l in links], [(l, 9) for l in links], (10, 11)),
-        12: ([(l, 6) for l in links], [], (12,)),
-        13: ([(l, 7) for l in links], [], (13,)),
-        14: ([(l, 8) for l in links], [], (14,)),
-        15: ([(l, 9) for l in links], [], (15,)),
+        1: (0, (2, 3, 4), (1, 2)),
+        3: (1, (), (3, 4)),
+        5: (2, (5, 6), (5,)),
+        6: (3, (7,), (6, 7)),
+        8: (4, (8,), (8, 9)),
+        10: (5, (9, 10), (10, 11)),
+        12: (6, (), (12,)),
+        13: (7, (), (13,)),
+        14: (8, (), (14,)),
     }
 
     def project_piece(step, plane):
@@ -182,25 +194,22 @@
         project(tokens, wflat, stage, src, half, ((q_ref, dst), (k_ref, dst), (v_ref, dst)))
 
     def pair_arrived(step):
-        for is_q in range(2):
-            pltpu.make_async_remote_copy(
-                src_ref=tokens.at[pl.ds(0, half)], dst_ref=tokens.at[pl.ds(0, half)], send_sem=pair_send_sem.at[0],
-                recv_sem=pair_sem.at[step, is_q], device_id=device(chip, other), device_id_type=MESH).wait_recv()
+        to_pair(tokens.at[pl.ds(0, 2 * half)], step).wait_recv()
 
     first = len(ORDER) - TAIL
 
     def body(s, _):
         step, sub = s // 2, lax.rem(s, 2)
-        for at, (waits, sends, pairs) in events.items():
+        for at, (wait, sends, pairs) in events.items():
             @pl.when(s == 2 * at)
-            def _(waits=waits, sends=sends, pairs=pairs):
-                for w in waits:
-                    arrived(*w)
-                for x in sends:
-                    send(*x)
+            def _(wait=wait, sends=sends, pairs=pairs):
+                arrived(wait)
+                for seq in sends:
+                    for link in links:
+                        send(link, seq)
                 for p in pairs:
-                    pair_copy(p, 0).start()
-                    pair_copy(p, 1).start()
+                    for copy in pair_copies(p):
+                        to_pair(*copy).start()
 
         @pl.when(jnp.logical_and(sub == 1, step > 0))
         def _():
@@ -211,17 +220,20 @@
             project_piece(step - sub, core + sub * (1 - 2 * core))
         return 0
 
-    lax.fori_loop(0, 2 * len(ORDER), body, 0)
-    pair_arrived(len(ORDER) - 1)
-
-    per_link = 5 * half + 5 * quarter
-    for link in links:
-        link_copy(link, 0, tokens.at[pl.ds(0, per_link)]).wait_send()
-    for i in range(4):
-        ref = tokens.at[pl.ds(0, 8 * half)]
-        pltpu.make_async_remote_copy(
-            src_ref=ref, dst_ref=ref, send_sem=pair_send_sem.at[i], recv_sem=pair_sem.at[0, 0],
-            device_id=device(chip, other), device_id_type=MESH).wait_send()
+    lax.fori_loop(0, 2 * len(ORDER) - 2, body, 0)
+
+    end = len(ORDER) - 1
+    for sub in range(2):
+        arrived(9 + sub)
+        for is_q in range(2):
+            for part in range(2):
+                to_pair(last_piece(end, is_q, part, sub), end + sub).start()
+    pair_arrived(end - 1)
+    for sub in range(2):
+        to_pair(tokens.at[pl.ds(0, half)], end + sub).wait_recv()
+
+    sent = 4 * (5 * half + 5 * quarter) + len(ORDER) * 2 * half
+    to_pair(tokens.at[pl.ds(0, sent)], 0).wait_send()
 
 
 def drain(side, rows, q_in, k_in, v_in, last, wflat, q_out, k_out, v_out, tail, stage, main_sem, tail_sem):
@@ -290,11 +302,10 @@
                 pltpu.VMEM((total, depth), jnp.bfloat16),
                 pltpu.VMEM((3, depth * heads, LANES), jnp.bfloat16),
                 pltpu.VMEM((3, rows * heads, LANES), jnp.float32),
-                pltpu.SemaphoreType.DMA((6,)),
                 pltpu.SemaphoreType.DMA((4,)),
-                pltpu.SemaphoreType.DMA((4,)),
-                pltpu.SemaphoreType.DMA((4, 10)),
-                pltpu.SemaphoreType.DMA((len(ORDER), 2)),
+                pltpu.SemaphoreType.DMA,
+                pltpu.SemaphoreType.DMA((11,)),
+                pltpu.SemaphoreType.DMA((len(ORDER) + 1,)),
             ],
             compiler_params=pltpu.CompilerParams(collective_id=0, has_side_effects=True, vmem_limit_bytes=50 * 1024 * 1024 // 2),
             name="gather_project",

time: 64 us -> 63.3 us (0.989)
  Pallas kernels: 63.3 us -> 62.6 us
    pallas_call x1, Pallas kernels: 54.9 us -> 54.2 us  [local_step(): pl.pallas_call(functools.partial(gather_project, side), out_shape=(vmem_o...]
where the time goes in v4:
time: 63.3 us; the launch traced here: 63.2 us
  Pallas kernels  62.6 us (99%)
  between operations  0.64 us (1%)
    pallas_call x1, Pallas kernels, local_step(): pl.pallas_call(functools.partial(gather_project, side), out_shape=(vmem_o...  54.2 us
    pallas_call x1, Pallas kernels, local_step(): pl.pallas_call(functools.partial(drain, side, rows), out_shape=(out,) * 3...  8.35 us

profile of v4, /device:TPU:97, one launch (start us, length us, event | category | flops | bytes accessed | tf_op | source)
XLA Modules:
  0.0 63.2 jit_solution(12510713493422172638)
XLA Ops:
  0.6 54.2 %gather_project.1 = (bf16[32768,128]{1,0:T(8,128)(2,1)S(1)}, bf16[32768,128]{1,0:T(8,128)(2,1)S(1)}, bf16[32768,128]{1,0:T(8,128)(2,1)S(1)}, bf16[1024,1024]{1,0:T(8,128)(2,1)S(1)}, bf16[1024,1536]{1,0:T(8,128)(2,1)S(1)}) custom-call(bf16[256,1024]{1,0:T(8,128)(2,1)} %x_hbm.1, f32[1,1024]{1,0:T(1,128)} %bitcast.10, bf16[4096,128]{1,0:T(8,128)(2,1)} %bitcast.7, ...), custom_call_target="tpu_custom_call" | custom-call | tf_op jit(solution)/shard_map/gather_project/pallas_call | solution.py:294
  54.9 8.4 %drain.1 = (bf16[32768,128]{1,0:T(8,128)(2,1)}, bf16[32768,128]{1,0:T(8,128)(2,1)}, bf16[32768,128]{1,0:T(8,128)(2,1)}) custom-call(bf16[32768,128]{1,0:T(8,128)(2,1)S(1)} %get-tuple-element.11.q_in, bf16[32768,128]{1,0:T(8,128)(2,1)S(1)} %get-tuple-element.12.k_in, bf16[32768,128]{1,0:T(8,128)(2,1)S(1)} %get-tuple-element.13.v_in, ...), custom_call_target="tpu_custom_call" | custom-call | tf_op jit(solution)/shard_map/drain/pallas_call | solution.py:314

commit v5 on v0

v5 whole, which is shorter than its diff:
```python
import functools
import math

import jax
import jax.numpy as jnp
from jax import lax
from jax.experimental import pallas as pl
from jax.experimental.pallas import tpu as pltpu
from jax.sharding import PartitionSpec as P

MESH = pl.DeviceIdType.MESH
CORES = 2
LANES = 128

DIRECT = ((0, 0), (-1, 0), (1, 0), (-1, 0), (1, 0), (2, 0), (-1, -1), (1, -1), (-1, 1), (1, 1), (-1, 2), (1, 2), (2, 0), (2, -1), (2, 1), (2, 2))
MINE = (0, 1, 2, 5)
STEPS = len(DIRECT)
TAIL = 3
PARTS = 4


class Place:
    def __init__(self, side):
        self.side = side
        me = lax.axis_index("tp")
        self.core = lax.rem(me, CORES)
        self.other = 1 - self.core
        self.chip = me // CORES
        self.x, self.y = lax.rem(self.chip, side), self.chip // side

    def chip_at(self, axis, u, v):
        dx, dy = u + axis * (v - u), v + axis * (u - v)
        return lax.rem(self.y + dy + self.side, self.side) * self.side + lax.rem(self.x + dx + self.side, self.side)

    def block(self, axis, step):
        u, v, mine = jnp.int32(0), jnp.int32(0), jnp.int32(0)
        for k, (ku, kv) in enumerate(DIRECT):
            u = jnp.where(step == k, ku, u)
            v = jnp.where(step == k, kv, v)
            mine = jnp.where(step == k, int(k in MINE), mine)
        return self.chip_at(axis, u, v) * CORES + axis + (1 - mine) * (1 - 2 * axis)


def project(lhs, wflat, stage, outs):
    rows = lhs.shape[0]
    heads = wflat.shape[1] // (3 * LANES)
    cols = heads * LANES
    for i, (out, dst) in enumerate(outs):
        for b in range(cols // 256):
            acc = jnp.dot(lhs, wflat[:, pl.ds(i * cols + b * 256, 256)], preferred_element_type=jnp.float32)
            for h in range(2):
                stage[i, pl.ds(b * 2 + h, rows, stride=heads), :] = acc[:, h * LANES:(h + 1) * LANES]
        out[pl.ds(dst, rows * heads), :] = stage[i].astype(jnp.bfloat16)


def gather_project(side, x_hbm, g_hbm, wq_hbm, wk_hbm, wv_hbm, q_ref, k_ref, v_ref, last, wflat, xbuf, g_ref, tokens, wraw, stage,
                   in_sem, send_sem, link_sem, pair_sem):
    rows, depth = xbuf.shape
    half, part = rows // 2, rows // 2 // PARTS
    heads = wraw.shape[1] // depth
    cols = heads * LANES
    first = STEPS - TAIL
    here = Place(side)
    core, other = here.core, here.other

    halves_in = [pltpu.make_async_copy(x_hbm.at[pl.ds(h * half, half)], xbuf.at[pl.ds(h * half, half)], in_sem.at[h]) for h in range(2)]
    gain_in = pltpu.make_async_copy(g_hbm, g_ref, in_sem.at[2])
    halves_in[0].start()
    gain_in.start()
    halves_in[1].start()

    next_to = [here.chip_at(core, d, 0) * CORES + core for d in (1, -1)]
    partner = here.chip * CORES + other
    barrier = pltpu.get_barrier_semaphore()
    for dev in (*next_to, partner):
        pl.semaphore_signal(barrier, inc=1, device_id={"tp": dev}, device_id_type=MESH)

    def rows_of(u, v, mine, start=0, count=rows):
        dev = here.chip_at(core, u, v) * CORES + (core if mine else other)
        return tokens.at[pl.ds(pl.multiple_of(dev * rows + start, part), count)]

    def rows_of_last(step, start=0, count=rows):
        return last.at[pl.ds(pl.multiple_of(((step - first) * CORES + core) * rows + start, part), count)]

    def link_copy(way, sem, src, dst):
        return pltpu.make_async_remote_copy(
            src_ref=src, dst_ref=dst, send_sem=send_sem, recv_sem=link_sem.at[sem], device_id={"tp": next_to[way]}, device_id_type=MESH)

    def pair_copy(sem, ref):
        return pltpu.make_async_remote_copy(
            src_ref=ref, dst_ref=ref, send_sem=send_sem, recv_sem=pair_sem.at[sem], device_id={"tp": partner}, device_id_type=MESH)

    def send(way, seq, start=0, count=rows):
        back = (-1, 1)[way]
        if seq in (2, 6, 7, 8, 9):
            start, count = way * half + start, min(count, half)
        u, v, mine = {0: (0, 0, 1), 1: (0, 0, 0), 2: (back, 0, 1), 3: (0, -1, 0), 4: (0, 1, 0), 5: (0, 2, 0),
                      6: (back, 0, 0), 7: (back, -1, 0), 8: (back, 1, 0), 9: (back, 2, 0)}[seq]
        src = rows_of(u, v, mine, start, count)
        step = STEPS - 10 + seq
        dst = rows_of_last(step, start, count) if step >= first else src
        sem = seq if seq < 9 else 9 + (start - way * half) // part
        link_copy(way, sem, src, dst).start()

    def arrived(sem, count):
        ref = tokens.at[pl.ds(0, 2 * count)]
        link_copy(0, sem, ref, ref).wait_recv()

    def pair_arrived(sem, count=rows):
        pair_copy(sem, tokens.at[pl.ds(0, count)]).wait_recv()

    def hand_over(step):
        if step >= first:
            ref = rows_of_last(step)
        else:
            ref = rows_of(*DIRECT[step], step in MINE)
        pair_copy(step, ref).start()

    own = (here.chip * CORES + core) * rows
    norm_rows = 32
    gain_in.wait()
    for h in range(2):
        halves_in[h].wait()
        if h == 0:
            for i, w in enumerate((wq_hbm, wk_hbm, wv_hbm)):
                pltpu.make_async_copy(w, wraw.at[i], in_sem.at[3]).start()
        for r in range(h * half, (h + 1) * half, norm_rows):
            xf = xbuf[pl.ds(r, norm_rows), :].astype(jnp.float32)
            mean_sq = jnp.mean(xf * xf, axis=-1, keepdims=True)
            n = (xf * lax.rsqrt(mean_sq + 1e-6) * g_ref[...]).astype(jnp.bfloat16)
            tokens[pl.ds(pl.multiple_of(own + r, norm_rows), norm_rows), :] = n
        if h == 0:
            pl.semaphore_wait(barrier, 3)
        for way in range(2):
            send(way, 0, h * half, half)
    hand_over(0)

    wrows = stage.shape[1] // heads
    pltpu.make_async_copy(wraw, wraw, in_sem.at[3]).wait()
    for i in range(3):
        def relayout(j, _, i=i):
            src = pl.multiple_of(j * (wrows * heads), wrows * heads)
            dst = pl.multiple_of(j * wrows, wrows)
            stage[i] = wraw[i, pl.ds(src, wrows * heads), :].astype(jnp.float32)
            for h in range(heads):
                wflat[pl.ds(dst, wrows), pl.ds(i * cols + h * LANES, LANES)] = stage[i, pl.ds(h, wrows, stride=heads), :].astype(jnp.bfloat16)
            return 0

        lax.fori_loop(0, depth // wrows, relayout, 0)

    turns = {
        1: ((), (0,), (), (1,)),
        2: ((0,), (), (1, 2), (2,)),
        4: ((), (1, 2), (), (3, 4)),
        6: ((1,), (), (3, 4), ()),
        10: ((2,), (), (5,), ()),
        12: ((3,), (), (6, 7), ()),
        13: ((), (5,), (), (5, 6, 7)),
        16: ((4,), (), (8, 9), (8,)),
        20: ((5,), (), (10, 11), (9,)),
        24: ((6,), (), (12,), ()),
        26: ((7,), (), (13,), ()),
        28: ((8,), (), (14,), ()),
    }
    for step in range(first):
        if step not in (0, 1, 2, 5):
            turns[2 * step + 3] = ((), (step,), (), ())

    def body(s, _):
        step, sub = s // 2, lax.rem(s, 2)
        for at, (links, pairs, handed, sends) in turns.items():
            @pl.when(s == at)
            def _(links=links, pairs=pairs, handed=handed, sends=sends):
                for seq in links:
                    arrived(seq, half if seq in (2, 6, 7, 8) else rows)
                for p in pairs:
                    pair_arrived(p)
                for seq in sends:
                    for i in range(PARTS if seq == 9 else 1):
                        for way in range(2):
                            if seq == 9:
                                send(way, seq, i * part, part)
                            else:
                                send(way, seq)
                for p in handed:
                    hand_over(p)

        @pl.when(jnp.where(sub == 0, step < first, jnp.logical_and(step > 0, step <= first)))
        def _():
            row = here.block(core + sub * (1 - 2 * core), step - sub) * rows
            lhs = tokens[pl.ds(pl.multiple_of(row, rows), rows), :]
            dst = pl.multiple_of(row * heads, rows * heads)
            project(lhs, wflat, stage, ((q_ref, dst), (k_ref, dst), (v_ref, dst)))
        return 0

    lax.fori_loop(0, 2 * STEPS - 3, body, 0)

    end = STEPS - 1
    for i in range(PARTS):
        arrived(9 + i, part)
        for way in range(2):
            pair_copy(end + i, rows_of_last(end, way * half + i * part, part)).start()
    for step in range(first, end):
        pair_arrived(step)
    for i in range(PARTS):
        pair_arrived(end + i, 2 * part)

    sent = 2 * (5 * rows + 5 * half) + STEPS * rows
    pair_copy(0, tokens.at[pl.ds(0, sent)]).wait_send()


def drain(side, rows, q_in, k_in, v_in, last, wflat, q_out, k_out, v_out, tail, stage, main_sem, tail_sem):
    ins, outs = (q_in, k_in, v_in), (q_out, k_out, v_out)
    heads = wflat.shape[1] // (3 * LANES)
    first = STEPS - TAIL
    here = Place(side)

    late = [{(u, v) if axis == 0 else (v, u) for u, v in DIRECT[first:]} for axis in (1, 0)]
    for dx, dy in sorted(set(DIRECT) | {(v, u) for u, v in DIRECT}):
        base = here.chip_at(0, dx, dy) * (CORES * rows)
        keep = [c for c in range(CORES) if (dx, dy) not in late[c]]
        if not keep:
            continue
        at = pl.ds(pl.multiple_of((base + keep[0] * rows) * heads, rows * heads), len(keep) * rows * heads)
        for i in range(3):
            pltpu.make_async_copy(ins[i].at[at], outs[i].at[at], main_sem.at[i]).start()

    def body(s, _):
        src = pl.multiple_of(s * rows, rows)
        mine = pl.ds(pl.multiple_of(s * (rows * heads), rows * heads), rows * heads)
        dst = pl.ds(pl.multiple_of(here.block(lax.rem(s, 2), first + s // 2) * (rows * heads), rows * heads), rows * heads)
        project(last[pl.ds(src, rows), :], wflat, stage, tuple((tail.at[i], src * heads) for i in range(3)))
        for i in range(3):
            pltpu.make_async_copy(tail.at[i, mine], outs[i].at[dst], tail_sem.at[i]).start()
        return 0

    lax.fori_loop(0, CORES * TAIL, body, 0)
    for i in range(3):
        n = first * CORES * rows * heads
        pltpu.make_async_copy(ins[i].at[pl.ds(0, n)], outs[i].at[pl.ds(0, n)], main_sem.at[i]).wait()
        pltpu.make_async_copy(tail.at[i], outs[i].at[pl.ds(0, CORES * TAIL * rows * heads)], tail_sem.at[i]).wait()


def solution(mesh):
    size = mesh.shape["tp"]
    side = math.isqrt(size // CORES)
    assert side * side * CORES == size and side * side == STEPS

    def local_step(x, gain, wq, wk, wv):
        rows, depth = x.shape
        heads = wq.shape[1]
        total = rows * size
        flat = [w.reshape(depth * heads, LANES) for w in (wq, wk, wv)]
        vmem_out = pltpu.VMEM((total * heads, LANES), jnp.bfloat16)
        outs = pl.pallas_call(
            functools.partial(gather_project, side),
            out_shape=(vmem_out,) * 3 + (pltpu.VMEM((TAIL * CORES * rows, depth), jnp.bfloat16), pltpu.VMEM((depth, 3 * heads * LANES), jnp.bfloat16)),
            in_specs=[pl.BlockSpec(memory_space=pltpu.HBM)] * 5,
            out_specs=[pl.BlockSpec(memory_space=pltpu.VMEM)] * 5,
            scratch_shapes=[
                pltpu.VMEM((rows, depth), jnp.bfloat16),
                pltpu.VMEM((1, depth), jnp.float32),
                pltpu.VMEM((total, depth), jnp.bfloat16),
                pltpu.VMEM((3, depth * heads, LANES), jnp.bfloat16),
                pltpu.VMEM((3, rows * heads, LANES), jnp.float32),
                pltpu.SemaphoreType.DMA((4,)),
                pltpu.SemaphoreType.DMA,
                pltpu.SemaphoreType.DMA((9 + PARTS,)),
                pltpu.SemaphoreType.DMA((STEPS - 1 + PARTS,)),
            ],
            compiler_params=pltpu.CompilerParams(collective_id=0, has_side_effects=True, vmem_limit_bytes=98 * 1024 * 1024 // 4),
            name="gather_project",
        )(x, gain.reshape(1, depth), *flat)
        out = jax.ShapeDtypeStruct((total * heads, LANES), jnp.bfloat16)
        outs = pl.pallas_call(
            functools.partial(drain, side, rows),
            out_shape=(out,) * 3,
            in_specs=[pl.BlockSpec(memory_space=pltpu.VMEM)] * 5,
            out_specs=[pl.BlockSpec(memory_space=pl.ANY)] * 3,
            scratch_shapes=[
                pltpu.VMEM((3, TAIL * CORES * rows * heads, LANES), jnp.bfloat16),
                pltpu.VMEM((3, rows * heads, LANES), jnp.float32),
                pltpu.SemaphoreType.DMA((3,)),
                pltpu.SemaphoreType.DMA((3,)),
            ],
            compiler_params=pltpu.CompilerParams(vmem_limit_bytes=80 * 1024 * 1024 // 4),
            name="drain",
        )(*outs)
        return tuple(o.reshape(total, heads, LANES) for o in outs)

    row_spec = P(("dp", "tp"), None)
    head_spec = P(None, "tp", None)
    out_spec = P("dp", "tp", None)
    return jax.shard_map(local_step, mesh=mesh, in_specs=(row_spec, P(None), head_spec, head_spec, head_spec),
                         out_specs=(out_spec, out_spec, out_spec), check_vma=False)
```

time: 247 us -> 59.8 us (0.24)
  local copies, waits for them, and re-layouts: 120 us -> 0 us
  waiting for transfers between devices: 71.7 us -> 0 us
  Pallas kernels: 0 us -> 59.1 us
  matrix products: 37.6 us -> 0 us
  between operations: 14.1 us -> 0.64 us
  other arithmetic: 3.34 us -> 0 us
    unnamed x11 -> x0, local copies, waits for them, and re-layouts: 120 us -> none
    all_gather x1 -> x0, waiting for transfers between devices: 71.7 us -> none  [local_step(): gathered = lax.all_gather(normed, 'tp', axis=0, tiled=True)]
    pallas_call x0 -> x2, Pallas kernels: none -> 59.1 us  [the longest x1 50.7 us: local_step(): pl.pallas_call(functools.partial(gather_project, side), out_shape=(vmem_o...]
    dot_general x3 -> x0, matrix products: 37.6 us -> none  [the longest x1 12.6 us: local_step(): jnp.einsum('td,dhk->thk', gathered, wv_local, preferred_element_type=jnp....]
  transfers between devices with their start and end apart: 1 -> 0, of which waited for: 1 -> 0; matrix products, arithmetic and copies ran while one was open for 0% -> 0% of each run, Pallas kernels for 0% -> 0%
where the time goes in v5:
time: 59.8 us; the launch traced here: 59.7 us
  Pallas kernels  59.1 us (99%)
  between operations  0.64 us (1%)
    pallas_call x1, Pallas kernels, local_step(): pl.pallas_call(functools.partial(gather_project, side), out_shape=(vmem_o...  50.7 us
    pallas_call x1, Pallas kernels, local_step(): pl.pallas_call(functools.partial(drain, side, rows), out_shape=(out,) * 3...  8.37 us

profile of v5, /device:TPU:97, one launch (start us, length us, event | category | flops | bytes accessed | tf_op | source)
XLA Modules:
  0.0 59.7 jit_solution(5210960271466648777)
XLA Ops:
  0.6 50.7 %gather_project.1 = (bf16[32768,128]{1,0:T(8,128)(2,1)S(1)}, bf16[32768,128]{1,0:T(8,128)(2,1)S(1)}, bf16[32768,128]{1,0:T(8,128)(2,1)S(1)}, bf16[1536,1024]{1,0:T(8,128)(2,1)S(1)}, bf16[1024,1536]{1,0:T(8,128)(2,1)S(1)}) custom-call(bf16[256,1024]{1,0:T(8,128)(2,1)} %x_hbm.1, f32[1,1024]{1,0:T(1,128)} %bitcast.10, bf16[4096,128]{1,0:T(8,128)(2,1)} %bitcast.7, ...), custom_call_target="tpu_custom_call" | custom-call | tf_op jit(solution)/shard_map/gather_project/pallas_call | solution.py:255
  51.4 8.4 %drain.1 = (bf16[32768,128]{1,0:T(8,128)(2,1)}, bf16[32768,128]{1,0:T(8,128)(2,1)}, bf16[32768,128]{1,0:T(8,128)(2,1)}) custom-call(bf16[32768,128]{1,0:T(8,128)(2,1)S(1)} %get-tuple-element.11.q_in, bf16[32768,128]{1,0:T(8,128)(2,1)S(1)} %get-tuple-element.12.k_in, bf16[32768,128]{1,0:T(8,128)(2,1)S(1)} %get-tuple-element.13.v_in, ...), custom_call_target="tpu_custom_call" | custom-call | tf_op jit(solution)/shard_map/drain/pallas_call | solution.py:275

commit v6 on v5

--- a/solution.py
+++ b/solution.py
@@ -15,8 +15,10 @@
 DIRECT = ((0, 0), (-1, 0), (1, 0), (-1, 0), (1, 0), (2, 0), (-1, -1), (1, -1), (-1, 1), (1, 1), (-1, 2), (1, 2), (2, 0), (2, -1), (2, 1), (2, 2))
 MINE = (0, 1, 2, 5)
 STEPS = len(DIRECT)
+PAIR_SEM = {0: 0, 1: 1, 2: 1, 3: 2, 4: 2, 5: 3, 6: 4, 7: 4, 8: 5, 9: 5, 10: 6, 11: 6, 12: 7, 13: 8, 14: 8, 15: 8}
 TAIL = 3
-PARTS = 4
+PARTS = 8
+X_PARTS = 8
 
 
 class Place:
@@ -63,11 +65,13 @@
     here = Place(side)
     core, other = here.core, here.other
 
-    halves_in = [pltpu.make_async_copy(x_hbm.at[pl.ds(h * half, half)], xbuf.at[pl.ds(h * half, half)], in_sem.at[h]) for h in range(2)]
-    gain_in = pltpu.make_async_copy(g_hbm, g_ref, in_sem.at[2])
-    halves_in[0].start()
+    few = rows // X_PARTS
+    x_in = [pltpu.make_async_copy(x_hbm.at[pl.ds(h * few, few)], xbuf.at[pl.ds(h * few, few)], in_sem.at[2 + h]) for h in range(X_PARTS)]
+    gain_in = pltpu.make_async_copy(g_hbm, g_ref, in_sem.at[0])
+    x_in[0].start()
     gain_in.start()
-    halves_in[1].start()
+    for copy in x_in[1:]:
+        copy.start()
 
     next_to = [here.chip_at(core, d, 0) * CORES + core for d in (1, -1)]
     partner = here.chip * CORES + other
@@ -86,9 +90,9 @@
         return pltpu.make_async_remote_copy(
             src_ref=src, dst_ref=dst, send_sem=send_sem, recv_sem=link_sem.at[sem], device_id={"tp": next_to[way]}, device_id_type=MESH)
 
-    def pair_copy(sem, ref):
+    def pair_copy(step, ref):
         return pltpu.make_async_remote_copy(
-            src_ref=ref, dst_ref=ref, send_sem=send_sem, recv_sem=pair_sem.at[sem], device_id={"tp": partner}, device_id_type=MESH)
+            src_ref=ref, dst_ref=ref, send_sem=send_sem, recv_sem=pair_sem.at[PAIR_SEM[step]], device_id={"tp": partner}, device_id_type=MESH)
 
     def send(way, seq, start=0, count=rows):
         back = (-1, 1)[way]
@@ -106,8 +110,9 @@
         ref = tokens.at[pl.ds(0, 2 * count)]
         link_copy(0, sem, ref, ref).wait_recv()
 
-    def pair_arrived(sem, count=rows):
-        pair_copy(sem, tokens.at[pl.ds(0, count)]).wait_recv()
+    def pair_arrived(step):
+        together = sum(sem == PAIR_SEM[step] for sem in PAIR_SEM.values())
+        pair_copy(step, tokens.at[pl.ds(0, together * rows)]).wait_recv()
 
     def hand_over(step):
         if step >= first:
@@ -119,12 +124,12 @@
     own = (here.chip * CORES + core) * rows
     norm_rows = 32
     gain_in.wait()
-    for h in range(2):
-        halves_in[h].wait()
-        if h == 0:
+    for h in range(X_PARTS):
+        x_in[h].wait()
+        if h == X_PARTS - 1:
             for i, w in enumerate((wq_hbm, wk_hbm, wv_hbm)):
-                pltpu.make_async_copy(w, wraw.at[i], in_sem.at[3]).start()
-        for r in range(h * half, (h + 1) * half, norm_rows):
+                pltpu.make_async_copy(w, wraw.at[i], in_sem.at[1]).start()
+        for r in range(h * few, (h + 1) * few, norm_rows):
             xf = xbuf[pl.ds(r, norm_rows), :].astype(jnp.float32)
             mean_sq = jnp.mean(xf * xf, axis=-1, keepdims=True)
             n = (xf * lax.rsqrt(mean_sq + 1e-6) * g_ref[...]).astype(jnp.bfloat16)
@@ -132,11 +137,11 @@
         if h == 0:
             pl.semaphore_wait(barrier, 3)
         for way in range(2):
-            send(way, 0, h * half, half)
+            send(way, 0, h * few, few)
     hand_over(0)
 
     wrows = stage.shape[1] // heads
-    pltpu.make_async_copy(wraw, wraw, in_sem.at[3]).wait()
+    pltpu.make_async_copy(wraw, wraw, in_sem.at[1]).wait()
     for i in range(3):
         def relayout(j, _, i=i):
             src = pl.multiple_of(j * (wrows * heads), wrows * heads)
@@ -149,32 +154,31 @@
         lax.fori_loop(0, depth // wrows, relayout, 0)
 
     turns = {
-        1: ((), (0,), (), (1,)),
-        2: ((0,), (), (1, 2), (2,)),
-        4: ((), (1, 2), (), (3, 4)),
-        6: ((1,), (), (3, 4), ()),
-        10: ((2,), (), (5,), ()),
-        12: ((3,), (), (6, 7), ()),
-        13: ((), (5,), (), (5, 6, 7)),
-        16: ((4,), (), (8, 9), (8,)),
-        20: ((5,), (), (10, 11), (9,)),
-        24: ((6,), (), (12,), ()),
-        26: ((7,), (), (13,), ()),
-        28: ((8,), (), (14,), ()),
+        1: ((), 0, (), (1,)),
+        2: ((0,), None, (1, 2), (2,)),
+        4: ((), 1, (), (3, 4)),
+        6: ((1,), None, (3, 4), ()),
+        10: ((2,), None, (5,), ()),
+        12: ((3,), None, (6, 7), ()),
+        13: ((), 5, (), (5, 6, 7)),
+        16: ((4,), None, (8, 9), (8,)),
+        20: ((5,), None, (10, 11), (9,)),
+        24: ((6,), None, (12,), ()),
+        26: ((7,), None, (13,), ()),
+        28: ((8,), None, (14,), ()),
     }
-    for step in range(first):
-        if step not in (0, 1, 2, 5):
-            turns[2 * step + 3] = ((), (step,), (), ())
+    for step in (3, 6, 8, 10, 12):
+        turns[2 * step + 3] = ((), step, (), ())
 
     def body(s, _):
         step, sub = s // 2, lax.rem(s, 2)
-        for at, (links, pairs, handed, sends) in turns.items():
+        for at, (links, pair, handed, sends) in turns.items():
             @pl.when(s == at)
-            def _(links=links, pairs=pairs, handed=handed, sends=sends):
+            def _(links=links, pair=pair, handed=handed, sends=sends):
                 for seq in links:
                     arrived(seq, half if seq in (2, 6, 7, 8) else rows)
-                for p in pairs:
-                    pair_arrived(p)
+                if pair is not None:
+                    pair_arrived(pair)
                 for seq in sends:
                     for i in range(PARTS if seq == 9 else 1):
                         for way in range(2):
@@ -199,11 +203,8 @@
     for i in range(PARTS):
         arrived(9 + i, part)
         for way in range(2):
-            pair_copy(end + i, rows_of_last(end, way * half + i * part, part)).start()
-    for step in range(first, end):
-        pair_arrived(step)
-    for i in range(PARTS):
-        pair_arrived(end + i, 2 * part)
+            pair_copy(end, rows_of_last(end, way * half + i * part, part)).start()
+    pair_arrived(end)
 
     sent = 2 * (5 * rows + 5 * half) + STEPS * rows
     pair_copy(0, tokens.at[pl.ds(0, sent)]).wait_send()
@@ -263,10 +264,10 @@
                 pltpu.VMEM((total, depth), jnp.bfloat16),
                 pltpu.VMEM((3, depth * heads, LANES), jnp.bfloat16),
                 pltpu.VMEM((3, rows * heads, LANES), jnp.float32),
-                pltpu.SemaphoreType.DMA((4,)),
+                pltpu.SemaphoreType.DMA((2 + X_PARTS,)),
                 pltpu.SemaphoreType.DMA,
                 pltpu.SemaphoreType.DMA((9 + PARTS,)),
-                pltpu.SemaphoreType.DMA((STEPS - 1 + PARTS,)),
+                pltpu.SemaphoreType.DMA((max(PAIR_SEM.values()) + 1,)),
             ],
             compiler_params=pltpu.CompilerParams(collective_id=0, has_side_effects=True, vmem_limit_bytes=98 * 1024 * 1024 // 4),
             name="gather_project",

time: 59.8 us -> 59.6 us (level)
  no operation moved by 1% of the time
where the time goes in v6:
time: 59.6 us; the launch traced here: 59.5 us
  Pallas kernels  58.8 us (99%)
  between operations  0.64 us (1%)
    pallas_call x1, Pallas kernels, local_step(): pl.pallas_call(functools.partial(gather_project, side), out_shape=(vmem_o...  50.5 us
    pallas_call x1, Pallas kernels, local_step(): pl.pallas_call(functools.partial(drain, side, rows), out_shape=(out,) * 3...  8.37 us

profile of v6, /device:TPU:97, one launch (start us, length us, event | category | flops | bytes accessed | tf_op | source)
XLA Modules:
  0.0 59.5 jit_solution(419466837755938899)
XLA Ops:
  0.6 50.5 %gather_project.1 = (bf16[32768,128]{1,0:T(8,128)(2,1)S(1)}, bf16[32768,128]{1,0:T(8,128)(2,1)S(1)}, bf16[32768,128]{1,0:T(8,128)(2,1)S(1)}, bf16[1536,1024]{1,0:T(8,128)(2,1)S(1)}, bf16[1024,1536]{1,0:T(8,128)(2,1)S(1)}) custom-call(bf16[256,1024]{1,0:T(8,128)(2,1)} %x_hbm.1, f32[1,1024]{1,0:T(1,128)} %bitcast.10, bf16[4096,128]{1,0:T(8,128)(2,1)} %bitcast.7, ...), custom_call_target="tpu_custom_call" | custom-call | tf_op jit(solution)/shard_map/gather_project/pallas_call | solution.py:256
  51.1 8.4 %drain.1 = (bf16[32768,128]{1,0:T(8,128)(2,1)}, bf16[32768,128]{1,0:T(8,128)(2,1)}, bf16[32768,128]{1,0:T(8,128)(2,1)}) custom-call(bf16[32768,128]{1,0:T(8,128)(2,1)S(1)} %get-tuple-element.11.q_in, bf16[32768,128]{1,0:T(8,128)(2,1)S(1)} %get-tuple-element.12.k_in, bf16[32768,128]{1,0:T(8,128)(2,1)S(1)} %get-tuple-element.13.v_in, ...), custom_call_target="tpu_custom_call" | custom-call | tf_op jit(solution)/shard_map/drain/pallas_call | solution.py:276

commit v7 on v6

--- a/solution.py
+++ b/solution.py
@@ -17,7 +17,7 @@
 STEPS = len(DIRECT)
 PAIR_SEM = {0: 0, 1: 1, 2: 1, 3: 2, 4: 2, 5: 3, 6: 4, 7: 4, 8: 5, 9: 5, 10: 6, 11: 6, 12: 7, 13: 8, 14: 8, 15: 8}
 TAIL = 3
-PARTS = 8
+PARTS = 4
 X_PARTS = 8
 
 
@@ -56,7 +56,7 @@
 
 
 def gather_project(side, x_hbm, g_hbm, wq_hbm, wk_hbm, wv_hbm, q_ref, k_ref, v_ref, last, wflat, xbuf, g_ref, tokens, wraw, stage,
-                   in_sem, send_sem, link_sem, pair_sem):
+                   in_sem, send_sem, link_sem, pair_sem, cross_sem):
     rows, depth = xbuf.shape
     half, part = rows // 2, rows // 2 // PARTS
     heads = wraw.shape[1] // depth
@@ -89,6 +89,10 @@
     def link_copy(way, sem, src, dst):
         return pltpu.make_async_remote_copy(
             src_ref=src, dst_ref=dst, send_sem=send_sem, recv_sem=link_sem.at[sem], device_id={"tp": next_to[way]}, device_id_type=MESH)
+
+    def cross_copy(way, ref):
+        return pltpu.make_async_remote_copy(
+            src_ref=ref[0], dst_ref=ref[1], send_sem=send_sem, recv_sem=cross_sem, device_id={"tp": next_to[way] + other - core}, device_id_type=MESH)
 
     def pair_copy(step, ref):
         return pltpu.make_async_remote_copy(
@@ -105,6 +109,8 @@
         dst = rows_of_last(step, start, count) if step >= first else src
         sem = seq if seq < 9 else 9 + (start - way * half) // part
         link_copy(way, sem, src, dst).start()
+        if sem == 8 + PARTS:
+            cross_copy(way, (src, dst)).start()
 
     def arrived(sem, count):
         ref = tokens.at[pl.ds(0, 2 * count)]
@@ -112,7 +118,8 @@
 
     def pair_arrived(step):
         together = sum(sem == PAIR_SEM[step] for sem in PAIR_SEM.values())
-        pair_copy(step, tokens.at[pl.ds(0, together * rows)]).wait_recv()
+        crossed = 2 * part if step == STEPS - 1 else 0
+        pair_copy(step, tokens.at[pl.ds(0, together * rows - crossed)]).wait_recv()
 
     def hand_over(step):
         if step >= first:
@@ -202,9 +209,11 @@
     end = STEPS - 1
     for i in range(PARTS):
         arrived(9 + i, part)
-        for way in range(2):
+        for way in range(2 if i < PARTS - 1 else 0):
             pair_copy(end, rows_of_last(end, way * half + i * part, part)).start()
     pair_arrived(end)
+    cross = tokens.at[pl.ds(0, 2 * part)]
+    cross_copy(0, (cross, cross)).wait_recv()
 
     sent = 2 * (5 * rows + 5 * half) + STEPS * rows
     pair_copy(0, tokens.at[pl.ds(0, sent)]).wait_send()
@@ -268,6 +277,7 @@
                 pltpu.SemaphoreType.DMA,
                 pltpu.SemaphoreType.DMA((9 + PARTS,)),
                 pltpu.SemaphoreType.DMA((max(PAIR_SEM.values()) + 1,)),
+                pltpu.SemaphoreType.DMA,
             ],
             compiler_params=pltpu.CompilerParams(collective_id=0, has_side_effects=True, vmem_limit_bytes=98 * 1024 * 1024 // 4),
             name="gather_project",

time: 59.6 us -> 59.3 us (level)
  no operation moved by 1% of the time
where the time goes in v7:
time: 59.3 us; the launch traced here: 59.1 us
  Pallas kernels  58.5 us (99%)
  between operations  0.64 us (1%)
    pallas_call x1, Pallas kernels, local_step(): pl.pallas_call(functools.partial(gather_project, side), out_shape=(vmem_o...  50.1 us
    pallas_call x1, Pallas kernels, local_step(): pl.pallas_call(functools.partial(drain, side, rows), out_shape=(out,) * 3...  8.37 us

profile of v7, /device:TPU:97, one launch (start us, length us, event | category | flops | bytes accessed | tf_op | source)
XLA Modules:
  0.0 59.1 jit_solution(8605799831848873172)
XLA Ops:
  0.6 50.1 %gather_project.1 = (bf16[32768,128]{1,0:T(8,128)(2,1)S(1)}, bf16[32768,128]{1,0:T(8,128)(2,1)S(1)}, bf16[32768,128]{1,0:T(8,128)(2,1)S(1)}, bf16[1536,1024]{1,0:T(8,128)(2,1)S(1)}, bf16[1024,1536]{1,0:T(8,128)(2,1)S(1)}) custom-call(bf16[256,1024]{1,0:T(8,128)(2,1)} %x_hbm.1, f32[1,1024]{1,0:T(1,128)} %bitcast.10, bf16[4096,128]{1,0:T(8,128)(2,1)} %bitcast.7, ...), custom_call_target="tpu_custom_call" | custom-call | tf_op jit(solution)/shard_map/gather_project/pallas_call | solution.py:265
  50.8 8.4 %drain.1 = (bf16[32768,128]{1,0:T(8,128)(2,1)}, bf16[32768,128]{1,0:T(8,128)(2,1)}, bf16[32768,128]{1,0:T(8,128)(2,1)}) custom-call(bf16[32768,128]{1,0:T(8,128)(2,1)S(1)} %get-tuple-element.11.q_in, bf16[32768,128]{1,0:T(8,128)(2,1)S(1)} %get-tuple-element.12.k_in, bf16[32768,128]{1,0:T(8,128)(2,1)S(1)} %get-tuple-element.13.v_in, ...), custom_call_target="tpu_custom_call" | custom-call | tf_op jit(solution)/shard_map/drain/pallas_call | solution.py:286
